TPU v7x, 32 devices: a whole 2x2x4 slice. The times are simulated.
32 devices in a mesh: row: 4 (over z), col: 8 (over y, x, core).
Axes of the slice: x: 2, y: 2, z: 4, core: 2. Of those that a mesh axis runs over, the one named last changes fastest.
Arguments:
- tile_data: bfloat16 [8, 4, 8, 2, 128, 128], P(None, 'row', 'col'), may hold values from 0 to 1, as said below
- tile_cols: int32 [8, 4, 8, 2], P(None, 'row', 'col'), may hold values from -1 to 31, as said below
Outputs:
- vertex_triangles: float32 [8, 4, 128], P(None, 'row', 'col')
- triangles: float32 [], replicated
Inputs may be any that keep to these rules, and one draw needn't show every extreme that they name: `tile_cols`: slot (a, r, c, s) holds -1 (empty) or a tile column J with J % 8 == c and J >= a 4 + r; the columns of one tile row are distinct; every slot of tile row 0 is filled; tile row I keeps each slot that has an allowed column with probability (32 - I) / 32, so rows with a lower index hold more tiles on average. `tile_data`: entries are 0 or 1; tiles of empty slots are zero; a tile whose column equals its tile row is strictly upper triangular; about one entry in 8 of a stored tile is 1, with edges clustered among groups of vertices.
All inputs are finite; a program needn't handle non-finite values.
Results may differ from a plain program's by a relative error of at most 0.0003.
Values may be sent and summed in bfloat16 or wider, within the bound.
A program may use at most 128 MiB of HBM per device.

v0:
```python
import jax
import jax.numpy as jnp
from jax import lax
from jax.sharding import PartitionSpec as P

vertex_scale = 2.0 ** (-14)
total_scale = 2.0 ** (-12)


def taken_in(share, axis, dim):

    def gathered(part):
        return lax.all_gather(part, axis, axis=dim, tiled=True)

    return jax.tree.map(gathered, share)


def tile_counts(stored, middle, own_tiles, own_cols, col_tiles, col_index):
    valid = middle >= 0
    clipped = jnp.clip(middle, 0, col_tiles.shape[0] - 1).astype(jnp.int32)
    partner = col_tiles[clipped]
    partner_cols = col_index[clipped]
    matches = partner_cols[:, :, None] == own_cols[None, None, :]
    matches = matches & valid[:, None, None] & (own_cols >= 0)[None, None, :]
    weights = matches.astype(jnp.bfloat16)
    targets = jnp.einsum("pqs,sxz->pqxz", weights, own_tiles, preferred_element_type=jnp.float32)
    paths = jnp.einsum("pxy,pqyz->pqxz", stored, partner, preferred_element_type=jnp.float32)
    return jnp.sum(paths * targets, axis=(0, 1, 3))


def on_device(tile_data, tile_cols):
    rows_here = tile_data.shape[0]
    slots = tile_data.shape[3]
    width = tile_data.shape[4]
    own_tiles = tile_data[:, 0, 0]
    own_cols = tile_cols[:, 0, 0]
    row_index = lax.all_gather(tile_cols, "col", axis=2, tiled=True)
    col_index = lax.all_gather(tile_cols, "row", axis=1, tiled=True)
    col_tiles = lax.all_gather(tile_data, "row", axis=1, tiled=True)
    tile_rows = col_index.shape[0] * col_index.shape[1]
    col_index = col_index.reshape(tile_rows, slots)
    col_tiles = col_tiles.reshape(tile_rows, slots, width, width)

    def add_piece(carry, piece, start):
        devices_here = piece.shape[2]
        middle = lax.dynamic_slice_in_dim(row_index, start.astype(jnp.int32), devices_here, 2)
        middle = middle.reshape(rows_here, devices_here * slots)
        stored = piece.reshape(rows_here, devices_here * slots, width, width)

        def per_row(packed):
            return tile_counts(packed[0], packed[1], packed[2], packed[3], col_tiles, col_index)

        return carry + lax.map(per_row, (stored, middle, own_tiles, own_cols))

    initial = jnp.zeros((rows_here, width), jnp.float32)
    partial_value = add_piece(initial, taken_in(tile_data, "col", 2), jnp.int32(0))
    shares = lax.psum_scatter(
        partial_value.reshape(rows_here, 1, width), "col", scatter_dimension=2, tiled=True
    )
    vertices = tile_rows * width
    overall = lax.psum(jnp.sum(partial_value), ("row", "col"))
    return (shares * vertex_scale, overall * (total_scale / vertices))


def solution(mesh):
    return jax.shard_map(
        on_device,
        mesh=mesh,
        in_specs=(P(None, "row", "col", None, None, None), P(None, "row", "col", None)),
        out_specs=(P(None, "row", "col"), P()),
        check_vma=False,
    )
```

profile of v0, /device:TPU:0, one launch (start us, length us, event | category | flops | bytes accessed | tf_op | source)
XLA Modules:
  0.0 213.6 jit_solution(9713125407251959521)
XLA Ops:
  7.2 0.7 all-gather.3.cloned.1.call-update
  8.0 0.7 all-gather.5.cloned.1.call-update
  8.7 2.4 %copy.37 = bf16[8,1,1,2,128,128]{5,3,4,0,2,1:T(2,128)(2,1)} copy(bf16[8,1,1,2,128,128]{5,4,3,2,1,0:T(8,128)(2,1)} %param.4) | data formatting | bytes 1048576 | tf_op args[0]
  11.1 12.6 %all_gather.15 = s32[8,4,1,2]{0,3,2,1:T(2,128)S(1)} all-gather(s32[8,1,1,2]{0,3,2,1:T(2,128)S(1)} %copy-done.1), channel_id=1, replica_groups=mesh['row'=4,'col'=8] {'row'}, dimensions={1}, use_global_device_ids=true | all-gather | bytes 320 | tf_op jit(solution)/shard_map/all_gather | solution.py:38
  23.8 0.1 copy.32
  23.9 8.9 %all_gather.12 = s32[8,1,8,2]{0,3,1,2:T(2,128)S(1)} all-gather(s32[8,1,1,2]{0,3,1,2:T(2,128)S(1)} %bitcast.68), channel_id=1, replica_groups=mesh['row'=4,'col'=8] {'col'}, dimensions={2}, use_global_device_ids=true | all-gather | bytes 576 | tf_op jit(solution)/shard_map/all_gather | solution.py:37
  33.0 25.0 %all-gather.3.cloned.1.call-done = bf16[8,4,1,2,128,128]{5,4,3,2,1,0:T(8,128)(2,1)} async-done(((bf16[8,1,1,2,128,128]{5,4,3,2,1,0:T(8,128)(2,1)}), bf16[8,4,1,2,128,128]{5,4,3,2,1,0:T(8,128)(2,1)}) %all-gather.3.cloned.1.call-update) | async-done | bytes 2097168 | tf_op jit(solution)/shard_map/all_gather | solution.py:39
  58.0 37.3 %all-gather.5.cloned.1.call-done = bf16[8,1,8,2,128,128]{5,4,3,2,1,0:T(8,128)(2,1)} async-done(((bf16[8,1,1,2,128,128]{5,4,3,2,1,0:T(8,128)(2,1)}), bf16[8,1,8,2,128,128]{5,4,3,2,1,0:T(8,128)(2,1)}) %all-gather.5.cloned.1.call-update) | async-done | bytes 4194320 | tf_op jit(solution)/shard_map/all_gather | solution.py:13
  95.3 67.3 %while.10 = (s32[]{:T(128)}, f32[8,128]{1,0:T(8,128)S(1)}, s32[8,16]{1,0:T(8,128)S(1)}, bf16[32,2,128,128]{3,2,1,0:T(8,128)(2,1)}, bf16[8,16,128,128]{3,2,1,0:T(...) while((s32[]{:T(128)}, f32[8,128]{1,0:T(8,128)S(1)}, ...), condition=%wide.region_2.3_spmd, body=%wide.region_0.2_spmd.sunk | while | flops 137364624 | bytes 20520652 | solution.py:53
  95.3 0.6 gather_fusion
  95.9 0.1 copy.40
  96.0 1.4 fusion.32
  97.4 1.8 copy.41
  99.3 2.5 %gather_fusion.1 = bf16[16,2,128,128]{3,2,1,0:T(8,128)(2,1)S(1)} fusion(bf16[32,2,128,128]{3,2,1,0:T(8,128)(2,1)} %get-tuple-element.163, s32[1024]{0:T(1024)S(1)} %pad_clamp_fusion.2), kind=kCustom, calls=%fused_computation.clone.1 | custom fusion | bytes 2097216 | tf_op jit(solution)/shard_map/while/body/eval_jaxpr/gather | solution.py:21
  101.8 1.9 fusion.33
  103.7 0.6 gather_fusion
  104.3 0.1 copy.40
  104.4 1.4 fusion.32
  105.8 1.8 copy.41
  107.7 2.5 %gather_fusion.1 = bf16[16,2,128,128]{3,2,1,0:T(8,128)(2,1)S(1)} fusion(bf16[32,2,128,128]{3,2,1,0:T(8,128)(2,1)} %get-tuple-element.163, s32[1024]{0:T(1024)S(1)} %pad_clamp_fusion.2), kind=kCustom, calls=%fused_computation.clone.1 | custom fusion | bytes 2097216 | tf_op jit(solution)/shard_map/while/body/eval_jaxpr/gather | solution.py:21
  110.2 1.9 fusion.33
  112.1 0.6 gather_fusion
  112.7 0.1 copy.40
  112.8 1.4 fusion.32
  114.3 1.8 copy.41
  116.1 2.5 %gather_fusion.1 = bf16[16,2,128,128]{3,2,1,0:T(8,128)(2,1)S(1)} fusion(bf16[32,2,128,128]{3,2,1,0:T(8,128)(2,1)} %get-tuple-element.163, s32[1024]{0:T(1024)S(1)} %pad_clamp_fusion.2), kind=kCustom, calls=%fused_computation.clone.1 | custom fusion | bytes 2097216 | tf_op jit(solution)/shard_map/while/body/eval_jaxpr/gather | solution.py:21
  118.6 1.9 fusion.33
  120.5 0.6 gather_fusion
  121.1 0.1 copy.40
  121.2 1.4 fusion.32
  122.7 1.8 copy.41
  124.5 2.5 %gather_fusion.1 = bf16[16,2,128,128]{3,2,1,0:T(8,128)(2,1)S(1)} fusion(bf16[32,2,128,128]{3,2,1,0:T(8,128)(2,1)} %get-tuple-element.163, s32[1024]{0:T(1024)S(1)} %pad_clamp_fusion.2), kind=kCustom, calls=%fused_computation.clone.1 | custom fusion | bytes 2097216 | tf_op jit(solution)/shard_map/while/body/eval_jaxpr/gather | solution.py:21
  127.0 1.9 fusion.33
  129.0 0.6 gather_fusion
  129.5 0.1 copy.40
  129.6 1.4 fusion.32
  131.1 1.8 copy.41
  132.9 2.5 %gather_fusion.1 = bf16[16,2,128,128]{3,2,1,0:T(8,128)(2,1)S(1)} fusion(bf16[32,2,128,128]{3,2,1,0:T(8,128)(2,1)} %get-tuple-element.163, s32[1024]{0:T(1024)S(1)} %pad_clamp_fusion.2), kind=kCustom, calls=%fused_computation.clone.1 | custom fusion | bytes 2097216 | tf_op jit(solution)/shard_map/while/body/eval_jaxpr/gather | solution.py:21
  135.4 1.9 fusion.33
  137.4 0.6 gather_fusion
  137.9 0.1 copy.40
  138.0 1.4 fusion.32
  139.5 1.8 copy.41
  141.3 2.5 %gather_fusion.1 = bf16[16,2,128,128]{3,2,1,0:T(8,128)(2,1)S(1)} fusion(bf16[32,2,128,128]{3,2,1,0:T(8,128)(2,1)} %get-tuple-element.163, s32[1024]{0:T(1024)S(1)} %pad_clamp_fusion.2), kind=kCustom, calls=%fused_computation.clone.1 | custom fusion | bytes 2097216 | tf_op jit(solution)/shard_map/while/body/eval_jaxpr/gather | solution.py:21
  143.8 1.9 fusion.33
  145.8 0.6 gather_fusion
  146.3 0.1 copy.40
  146.4 1.4 fusion.32
  147.9 1.8 copy.41
  149.7 2.5 %gather_fusion.1 = bf16[16,2,128,128]{3,2,1,0:T(8,128)(2,1)S(1)} fusion(bf16[32,2,128,128]{3,2,1,0:T(8,128)(2,1)} %get-tuple-element.163, s32[1024]{0:T(1024)S(1)} %pad_clamp_fusion.2), kind=kCustom, calls=%fused_computation.clone.1 | custom fusion | bytes 2097216 | tf_op jit(solution)/shard_map/while/body/eval_jaxpr/gather | solution.py:21
  152.2 1.9 fusion.33
  154.2 0.6 gather_fusion
  154.8 0.1 copy.40
  154.9 1.4 fusion.32
  156.3 1.8 copy.41
  158.2 2.5 %gather_fusion.1 = bf16[16,2,128,128]{3,2,1,0:T(8,128)(2,1)S(1)} fusion(bf16[32,2,128,128]{3,2,1,0:T(8,128)(2,1)} %get-tuple-element.163, s32[1024]{0:T(1024)S(1)} %pad_clamp_fusion.2), kind=kCustom, calls=%fused_computation.clone.1 | custom fusion | bytes 2097216 | tf_op jit(solution)/shard_map/while/body/eval_jaxpr/gather | solution.py:21
  160.7 1.9 fusion.33
  162.6 0.3 copy.33
  162.8 0.8 bitcast_reduce_fusion
  163.7 0.6 reduce_sum.18
  164.3 39.5 %psum.7 = f32[]{:T(128)} all-reduce(f32[]{:T(128)} %reduce_sum.18), channel_id=1, replica_groups=mesh['row'=4,'col'=8] {'row','col'}, use_global_device_ids=true, to_apply=%region_5.6 | all-reduce | flops 1 | bytes 8 | tf_op jit(solution)/shard_map/psum | solution.py:61
  204.4 0.8 reshape_bitcast_fusion
  205.2 0.1 copy.34
  205.3 0.6 broadcast_multiply_fusion
  (66 shorter events, 0.9 us)
Async XLA Ops:
  7.2 4.0 %copy-start.1 = (s32[8,1,1,2]{0,3,2,1:T(2,128)S(1)}, s32[8,1,1,2]{0,3,2,1:T(2,128)}, u32[]{:S(2)}) copy-start(s32[8,1,1,2]{0,3,2,1:T(2,128)} %param.5) | copy-start | bytes 196
  7.2 50.8 %all-gather.3.cloned.1.call-start = ((), (), s32[]{:S(2)}) async-start(), calls=%async_computation.1 | async-start | bytes 2621440 | tf_op jit(solution)/shard_map/all_gather | solution.py:39
  7.9 87.4 %all-gather.5.cloned.1.call-start = ((), (), s32[]{:S(2)}) async-start(), calls=%async_computation.2 | async-start | bytes 4718592 | tf_op jit(solution)/shard_map/all_gather | solution.py:13
  8.7 195.8 %reduce-scatter.4.cloned.1.call-start = ((), (), s32[]{:S(2)}) async-start(), calls=%async_computation.3 | async-start | bytes 73728
  99.3 2.5 %copy-start = (f32[16,2,128,128]{2,3,1,0:T(8,128)S(1)}, f32[16,2,128,128]{2,3,1,0:T(8,128)}, u32[]{:S(2)}) copy-start(f32[16,2,128,128]{2,3,1,0:T(8,128)} %copy.41) | copy-start | bytes 6291460 | tf_op jit(solution)/shard_map/while
  107.7 2.5 %copy-start = (f32[16,2,128,128]{2,3,1,0:T(8,128)S(1)}, f32[16,2,128,128]{2,3,1,0:T(8,128)}, u32[]{:S(2)}) copy-start(f32[16,2,128,128]{2,3,1,0:T(8,128)} %copy.41) | copy-start | bytes 6291460 | tf_op jit(solution)/shard_map/while
  116.1 2.5 %copy-start = (f32[16,2,128,128]{2,3,1,0:T(8,128)S(1)}, f32[16,2,128,128]{2,3,1,0:T(8,128)}, u32[]{:S(2)}) copy-start(f32[16,2,128,128]{2,3,1,0:T(8,128)} %copy.41) | copy-start | bytes 6291460 | tf_op jit(solution)/shard_map/while
  124.5 2.5 %copy-start = (f32[16,2,128,128]{2,3,1,0:T(8,128)S(1)}, f32[16,2,128,128]{2,3,1,0:T(8,128)}, u32[]{:S(2)}) copy-start(f32[16,2,128,128]{2,3,1,0:T(8,128)} %copy.41) | copy-start | bytes 6291460 | tf_op jit(solution)/shard_map/while
  132.9 2.5 %copy-start = (f32[16,2,128,128]{2,3,1,0:T(8,128)S(1)}, f32[16,2,128,128]{2,3,1,0:T(8,128)}, u32[]{:S(2)}) copy-start(f32[16,2,128,128]{2,3,1,0:T(8,128)} %copy.41) | copy-start | bytes 6291460 | tf_op jit(solution)/shard_map/while
  141.3 2.5 %copy-start = (f32[16,2,128,128]{2,3,1,0:T(8,128)S(1)}, f32[16,2,128,128]{2,3,1,0:T(8,128)}, u32[]{:S(2)}) copy-start(f32[16,2,128,128]{2,3,1,0:T(8,128)} %copy.41) | copy-start | bytes 6291460 | tf_op jit(solution)/shard_map/while
  149.7 2.5 %copy-start = (f32[16,2,128,128]{2,3,1,0:T(8,128)S(1)}, f32[16,2,128,128]{2,3,1,0:T(8,128)}, u32[]{:S(2)}) copy-start(f32[16,2,128,128]{2,3,1,0:T(8,128)} %copy.41) | copy-start | bytes 6291460 | tf_op jit(solution)/shard_map/while
  158.2 2.5 %copy-start = (f32[16,2,128,128]{2,3,1,0:T(8,128)S(1)}, f32[16,2,128,128]{2,3,1,0:T(8,128)}, u32[]{:S(2)}) copy-start(f32[16,2,128,128]{2,3,1,0:T(8,128)} %copy.41) | copy-start | bytes 6291460 | tf_op jit(solution)/shard_map/while
Sparse Core Ops, SparseCore 0:
  9.6 48.3 all-gather.2
  59.9 35.3 all-gather.4
  163.8 33.5 reduce-scatter.3
where the time goes:
time: 215 us; the launch traced here: 214 us
  waiting for transfers between devices  63.7 us (30%)
  blocking collectives  61 us (28%)
  local copies, waits for them, and re-layouts  44.8 us (21%)
  matrix products  26.4 us (12%)
  between operations  15.6 us (7%)
    psum x1, blocking collectives, on_device(): overall = lax.psum(jnp.sum(partial_value), ('row', 'col'))  39.5 us
    all_gather x1, waiting for transfers between devices, gathered(): return lax.all_gather(part, axis, axis=dim, tiled=True)  37.3 us
    all_gather x1, waiting for transfers between devices, on_device(): col_tiles = lax.all_gather(tile_data, 'row', axis=1, tiled=True)  25 us
    gather x8, local copies, waits for them, and re-layouts, tile_counts(): partner = col_tiles[clipped]  19.9 us
    dot_general x8, matrix products, tile_counts(): jnp.einsum('pxy,pqyz->pqxz', stored, partner, preferred_element_type=jnp....  14.9 us
    dot_general x8, local copies, waits for them, and re-layouts, tile_counts(): jnp.einsum('pqs,sxz->pqxz', weights, own_tiles, preferred_element_type=jn...  14.7 us
    all_gather x1, blocking collectives, on_device(): col_index = lax.all_gather(tile_cols, 'row', axis=1, tiled=True)  12.6 us
    dot_general x8, matrix products, tile_counts(): jnp.einsum('pqs,sxz->pqxz', weights, own_tiles, preferred_element_type=jn...  11.5 us
  transfers between devices with their start and end apart: 3, of which 2 were waited for; matrix products, arithmetic and copies ran while one was open for 2% of the time, Pallas kernels for 0%

commit v1 on v0

--- a/solution.py
+++ b/solution.py
@@ -35,7 +35,9 @@
     own_tiles = tile_data[:, 0, 0]
     own_cols = tile_cols[:, 0, 0]
     row_index = lax.all_gather(tile_cols, "col", axis=2, tiled=True)
-    col_index = lax.all_gather(tile_cols, "row", axis=1, tiled=True)
+    col_index = jnp.concatenate(
+        lax.all_to_all(jnp.stack([tile_cols] * lax.axis_size("row")), "row", 0, 0), axis=1
+    )
     col_tiles = lax.all_gather(tile_data, "row", axis=1, tiled=True)
     tile_rows = col_index.shape[0] * col_index.shape[1]
     col_index = col_index.reshape(tile_rows, slots)

time: 215 us -> 215 us (level)
  blocking collectives: 61 us -> 48.4 us
  starting transfers between devices: 0.11 us -> 6.42 us
  waiting for transfers between devices: 63.7 us -> 68.1 us
    all_gather x1 -> x0, blocking collectives: 12.6 us -> none  [on_device(): col_index = lax.all_gather(tile_cols, 'row', axis=1, tiled=True)]
    all_to_all x0 -> x1, starting transfers between devices: none -> 6.35 us  [on_device(): lax.all_to_all(jnp.stack([tile_cols] * lax.axis_size('row')), 'row', 0, 0)]
    all_gather x1, waiting for transfers between devices: 25 us -> 29.4 us  [on_device(): col_tiles = lax.all_gather(tile_data, 'row', axis=1, tiled=True)]
  transfers between devices with their start and end apart: 3 -> 4, of which waited for: 2 -> 2; matrix products, arithmetic and copies ran while one was open for 2% -> 2% of each run, Pallas kernels for 0% -> 0%
where the time goes in v1:
time: 215 us; the launch traced here: 214 us
  waiting for transfers between devices  68.1 us (32%)
  blocking collectives  48.4 us (23%)
  local copies, waits for them, and re-layouts  46.7 us (22%)
  matrix products  26.4 us (12%)
  between operations  15.6 us (7%)
  starting transfers between devices  6.42 us (3%)
    psum x1, blocking collectives, on_device(): overall = lax.psum(jnp.sum(partial_value), ('row', 'col'))  39.5 us
    all_gather x1, waiting for transfers between devices, gathered(): return lax.all_gather(part, axis, axis=dim, tiled=True)  37.3 us
    all_gather x1, waiting for transfers between devices, on_device(): col_tiles = lax.all_gather(tile_data, 'row', axis=1, tiled=True)  29.4 us
    gather x8, local copies, waits for them, and re-layouts, tile_counts(): partner = col_tiles[clipped]  19.9 us
    dot_general x8, matrix products, tile_counts(): jnp.einsum('pxy,pqyz->pqxz', stored, partner, preferred_element_type=jnp....  14.9 us
    dot_general x8, local copies, waits for them, and re-layouts, tile_counts(): jnp.einsum('pqs,sxz->pqxz', weights, own_tiles, preferred_element_type=jn...  14.8 us
    dot_general x8, matrix products, tile_counts(): jnp.einsum('pqs,sxz->pqxz', weights, own_tiles, preferred_element_type=jn...  11.5 us
    all_gather x1, blocking collectives, on_device(): row_index = lax.all_gather(tile_cols, 'col', axis=2, tiled=True)  8.92 us
  transfers between devices with their start and end apart: 4, of which 2 were waited for; matrix products, arithmetic and copies ran while one was open for 2% of the time, Pallas kernels for 0%

profile of v1, /device:TPU:0, one launch (start us, length us, event | category | flops | bytes accessed | tf_op | source)
XLA Modules:
  0.0 213.6 jit_solution(8520755365105920007)
XLA Ops:
  7.2 0.7 all-gather.3.cloned.1.call-update
  8.0 0.7 all-gather.5.cloned.1.call-update
  8.7 1.3 stack.2
  9.9 6.3 %all-to-all-start = ((s32[4,8,1,1,2]{1,4,3,2,0:T(2,128)}), s32[4,8,1,1,2]{1,4,3,2,0:T(2,128)S(1)}, u32[]{:S(2)}, u32[]{:S(2)}) async-start(s32[4,8,1,1,2]{1,4,3,2,0:T(2,128)} %stack.2), calls=%async_computation | async-start | bytes 8192 | tf_op jit(solution)/shard_map/all_to_all | solution.py:39
  16.3 0.8 copy.26
  17.0 2.4 %copy.35 = bf16[8,1,1,2,128,128]{5,3,4,0,2,1:T(2,128)(2,1)} copy(bf16[8,1,1,2,128,128]{5,4,3,2,1,0:T(8,128)(2,1)} %param.4) | data formatting | bytes 1048576 | tf_op args[0]
  19.5 8.9 %all_gather.9 = s32[8,1,8,2]{0,3,1,2:T(2,128)S(1)} all-gather(s32[8,1,1,2]{0,3,1,2:T(2,128)S(1)} %bitcast.72), channel_id=1, replica_groups=mesh['row'=4,'col'=8] {'col'}, dimensions={2}, use_global_device_ids=true | all-gather | bytes 576 | tf_op jit(solution)/shard_map/all_gather | solution.py:37
  28.5 0.1 copy.30
  28.6 29.4 %all-gather.3.cloned.1.call-done = bf16[8,4,1,2,128,128]{5,4,3,2,1,0:T(8,128)(2,1)} async-done(((bf16[8,1,1,2,128,128]{5,4,3,2,1,0:T(8,128)(2,1)}), bf16[8,4,1,2,128,128]{5,4,3,2,1,0:T(8,128)(2,1)}) %all-gather.3.cloned.1.call-update) | async-done | bytes 2097168 | tf_op jit(solution)/shard_map/all_gather | solution.py:41
  58.0 37.3 %all-gather.5.cloned.1.call-done = bf16[8,1,8,2,128,128]{5,4,3,2,1,0:T(8,128)(2,1)} async-done(((bf16[8,1,1,2,128,128]{5,4,3,2,1,0:T(8,128)(2,1)}), bf16[8,1,8,2,128,128]{5,4,3,2,1,0:T(8,128)(2,1)}) %all-gather.5.cloned.1.call-update) | async-done | bytes 4194320 | tf_op jit(solution)/shard_map/all_gather | solution.py:13
  95.3 67.3 %while.10 = (s32[]{:T(128)}, f32[8,128]{1,0:T(8,128)S(1)}, s32[8,16]{1,0:T(8,128)S(1)}, bf16[32,2,128,128]{3,2,1,0:T(8,128)(2,1)}, bf16[8,16,128,128]{3,2,1,0:T(...) while((s32[]{:T(128)}, f32[8,128]{1,0:T(8,128)S(1)}, ...), condition=%wide.region_2.3_spmd, body=%wide.region_0.2_spmd.sunk | while | flops 137364624 | bytes 20520652 | solution.py:55
  95.3 0.6 gather_fusion
  95.9 0.1 copy.38
  96.0 1.4 fusion.32
  97.4 1.8 copy.39
  99.3 2.5 %gather_fusion.1 = bf16[16,2,128,128]{3,2,1,0:T(8,128)(2,1)S(1)} fusion(bf16[32,2,128,128]{3,2,1,0:T(8,128)(2,1)} %get-tuple-element.163, s32[1024]{0:T(1024)S(1)} %pad_clamp_fusion.2), kind=kCustom, calls=%fused_computation.clone.1 | custom fusion | bytes 2097216 | tf_op jit(solution)/shard_map/while/body/eval_jaxpr/gather | solution.py:21
  101.8 1.9 fusion.33
  103.7 0.6 gather_fusion
  104.3 0.1 copy.38
  104.4 1.4 fusion.32
  105.9 1.8 copy.39
  107.7 2.5 %gather_fusion.1 = bf16[16,2,128,128]{3,2,1,0:T(8,128)(2,1)S(1)} fusion(bf16[32,2,128,128]{3,2,1,0:T(8,128)(2,1)} %get-tuple-element.163, s32[1024]{0:T(1024)S(1)} %pad_clamp_fusion.2), kind=kCustom, calls=%fused_computation.clone.1 | custom fusion | bytes 2097216 | tf_op jit(solution)/shard_map/while/body/eval_jaxpr/gather | solution.py:21
  110.2 1.9 fusion.33
  112.1 0.6 gather_fusion
  112.7 0.1 copy.38
  112.8 1.4 fusion.32
  114.3 1.8 copy.39
  116.1 2.5 %gather_fusion.1 = bf16[16,2,128,128]{3,2,1,0:T(8,128)(2,1)S(1)} fusion(bf16[32,2,128,128]{3,2,1,0:T(8,128)(2,1)} %get-tuple-element.163, s32[1024]{0:T(1024)S(1)} %pad_clamp_fusion.2), kind=kCustom, calls=%fused_computation.clone.1 | custom fusion | bytes 2097216 | tf_op jit(solution)/shard_map/while/body/eval_jaxpr/gather | solution.py:21
  118.6 1.9 fusion.33
  120.6 0.6 gather_fusion
  121.1 0.1 copy.38
  121.2 1.4 fusion.32
  122.7 1.8 copy.39
  124.5 2.5 %gather_fusion.1 = bf16[16,2,128,128]{3,2,1,0:T(8,128)(2,1)S(1)} fusion(bf16[32,2,128,128]{3,2,1,0:T(8,128)(2,1)} %get-tuple-element.163, s32[1024]{0:T(1024)S(1)} %pad_clamp_fusion.2), kind=kCustom, calls=%fused_computation.clone.1 | custom fusion | bytes 2097216 | tf_op jit(solution)/shard_map/while/body/eval_jaxpr/gather | solution.py:21
  127.0 1.9 fusion.33
  129.0 0.6 gather_fusion
  129.6 1.4 fusion.32
  131.1 1.8 copy.39
  132.9 2.5 %gather_fusion.1 = bf16[16,2,128,128]{3,2,1,0:T(8,128)(2,1)S(1)} fusion(bf16[32,2,128,128]{3,2,1,0:T(8,128)(2,1)} %get-tuple-element.163, s32[1024]{0:T(1024)S(1)} %pad_clamp_fusion.2), kind=kCustom, calls=%fused_computation.clone.1 | custom fusion | bytes 2097216 | tf_op jit(solution)/shard_map/while/body/eval_jaxpr/gather | solution.py:21
  135.4 1.9 fusion.33
  137.4 0.6 gather_fusion
  138.1 1.4 fusion.32
  139.5 1.8 copy.39
  141.4 2.5 %gather_fusion.1 = bf16[16,2,128,128]{3,2,1,0:T(8,128)(2,1)S(1)} fusion(bf16[32,2,128,128]{3,2,1,0:T(8,128)(2,1)} %get-tuple-element.163, s32[1024]{0:T(1024)S(1)} %pad_clamp_fusion.2), kind=kCustom, calls=%fused_computation.clone.1 | custom fusion | bytes 2097216 | tf_op jit(solution)/shard_map/while/body/eval_jaxpr/gather | solution.py:21
  143.9 1.9 fusion.33
  145.8 0.6 gather_fusion
  146.4 0.1 copy.38
  146.5 1.4 fusion.32
  147.9 1.8 copy.39
  149.8 2.5 %gather_fusion.1 = bf16[16,2,128,128]{3,2,1,0:T(8,128)(2,1)S(1)} fusion(bf16[32,2,128,128]{3,2,1,0:T(8,128)(2,1)} %get-tuple-element.163, s32[1024]{0:T(1024)S(1)} %pad_clamp_fusion.2), kind=kCustom, calls=%fused_computation.clone.1 | custom fusion | bytes 2097216 | tf_op jit(solution)/shard_map/while/body/eval_jaxpr/gather | solution.py:21
  152.3 1.9 fusion.33
  154.2 0.6 gather_fusion
  154.8 0.1 copy.38
  154.9 1.4 fusion.32
  156.3 1.8 copy.39
  158.2 2.5 %gather_fusion.1 = bf16[16,2,128,128]{3,2,1,0:T(8,128)(2,1)S(1)} fusion(bf16[32,2,128,128]{3,2,1,0:T(8,128)(2,1)} %get-tuple-element.163, s32[1024]{0:T(1024)S(1)} %pad_clamp_fusion.2), kind=kCustom, calls=%fused_computation.clone.1 | custom fusion | bytes 2097216 | tf_op jit(solution)/shard_map/while/body/eval_jaxpr/gather | solution.py:21
  160.7 1.9 fusion.33
  162.6 0.3 copy.31
  162.8 0.8 bitcast_reduce_fusion
  163.7 0.6 reduce_sum.18
  164.3 39.5 %psum.7 = f32[]{:T(128)} all-reduce(f32[]{:T(128)} %reduce_sum.18), channel_id=1, replica_groups=mesh['row'=4,'col'=8] {'row','col'}, use_global_device_ids=true, to_apply=%region_5.6 | all-reduce | flops 1 | bytes 8 | tf_op jit(solution)/shard_map/psum | solution.py:63
  204.5 0.8 reshape_bitcast_fusion
  205.2 0.1 copy.32
  205.4 0.6 broadcast_multiply_fusion
  (68 shorter events, 1.0 us)
Async XLA Ops:
  7.2 12.3 %copy-start.1 = (s32[8,1,1,2]{0,3,2,1:T(2,128)S(1)}, s32[8,1,1,2]{0,3,2,1:T(2,128)}, u32[]{:S(2)}) copy-start(s32[8,1,1,2]{0,3,2,1:T(2,128)} %param.5) | copy-start | bytes 196
  7.2 50.8 %all-gather.3.cloned.1.call-start = ((), (), s32[]{:S(2)}) async-start(), calls=%async_computation.2 | async-start | bytes 2621440 | tf_op jit(solution)/shard_map/all_gather | solution.py:41
  7.9 87.4 %all-gather.5.cloned.1.call-start = ((), (), s32[]{:S(2)}) async-start(), calls=%async_computation.3 | async-start | bytes 4718592 | tf_op jit(solution)/shard_map/all_gather | solution.py:13
  9.9 18.5 %all-to-all-start = ((s32[4,8,1,1,2]{1,4,3,2,0:T(2,128)}), s32[4,8,1,1,2]{1,4,3,2,0:T(2,128)S(1)}, u32[]{:S(2)}, u32[]{:S(2)}) async-start(s32[4,8,1,1,2]{1,4,3,2,0:T(2,128)} %stack.2), calls=%async_computation | async-start | bytes 8192 | tf_op jit(solution)/shard_map/all_to_all | solution.py:39
  16.3 188.2 %reduce-scatter.4.cloned.1.call-start = ((), (), s32[]{:S(2)}) async-start(), calls=%async_computation.4 | async-start | bytes 73728
  99.3 2.5 %copy-start = (f32[16,2,128,128]{2,3,1,0:T(8,128)S(1)}, f32[16,2,128,128]{2,3,1,0:T(8,128)}, u32[]{:S(2)}) copy-start(f32[16,2,128,128]{2,3,1,0:T(8,128)} %copy.39) | copy-start | bytes 6291460 | tf_op jit(solution)/shard_map/while
  107.7 2.5 %copy-start = (f32[16,2,128,128]{2,3,1,0:T(8,128)S(1)}, f32[16,2,128,128]{2,3,1,0:T(8,128)}, u32[]{:S(2)}) copy-start(f32[16,2,128,128]{2,3,1,0:T(8,128)} %copy.39) | copy-start | bytes 6291460 | tf_op jit(solution)/shard_map/while
  116.1 2.5 %copy-start = (f32[16,2,128,128]{2,3,1,0:T(8,128)S(1)}, f32[16,2,128,128]{2,3,1,0:T(8,128)}, u32[]{:S(2)}) copy-start(f32[16,2,128,128]{2,3,1,0:T(8,128)} %copy.39) | copy-start | bytes 6291460 | tf_op jit(solution)/shard_map/while
  124.5 2.5 %copy-start = (f32[16,2,128,128]{2,3,1,0:T(8,128)S(1)}, f32[16,2,128,128]{2,3,1,0:T(8,128)}, u32[]{:S(2)}) copy-start(f32[16,2,128,128]{2,3,1,0:T(8,128)} %copy.39) | copy-start | bytes 6291460 | tf_op jit(solution)/shard_map/while
  132.9 2.5 %copy-start = (f32[16,2,128,128]{2,3,1,0:T(8,128)S(1)}, f32[16,2,128,128]{2,3,1,0:T(8,128)}, u32[]{:S(2)}) copy-start(f32[16,2,128,128]{2,3,1,0:T(8,128)} %copy.39) | copy-start | bytes 6291460 | tf_op jit(solution)/shard_map/while
  141.3 2.5 %copy-start = (f32[16,2,128,128]{2,3,1,0:T(8,128)S(1)}, f32[16,2,128,128]{2,3,1,0:T(8,128)}, u32[]{:S(2)}) copy-start(f32[16,2,128,128]{2,3,1,0:T(8,128)} %copy.39) | copy-start | bytes 6291460 | tf_op jit(solution)/shard_map/while
  149.8 2.5 %copy-start = (f32[16,2,128,128]{2,3,1,0:T(8,128)S(1)}, f32[16,2,128,128]{2,3,1,0:T(8,128)}, u32[]{:S(2)}) copy-start(f32[16,2,128,128]{2,3,1,0:T(8,128)} %copy.39) | copy-start | bytes 6291460 | tf_op jit(solution)/shard_map/while
  158.2 2.5 %copy-start = (f32[16,2,128,128]{2,3,1,0:T(8,128)S(1)}, f32[16,2,128,128]{2,3,1,0:T(8,128)}, u32[]{:S(2)}) copy-start(f32[16,2,128,128]{2,3,1,0:T(8,128)} %copy.39) | copy-start | bytes 6291460 | tf_op jit(solution)/shard_map/while
Sparse Core Ops, SparseCore 0:
  9.6 48.3 all-gather.2
  59.9 35.3 all-gather.4
  163.8 33.5 reduce-scatter.3
